TPU v7x, 32 devices: a whole 2x2x4 slice. The times are simulated.
32 devices in a mesh: groups: 2 (over y), space: 4 (over z), mp: 2 (over x), sub: 2 (over core).
Axes of the slice: x: 2, y: 2, z: 4, core: 2. Of those that a mesh axis runs over, the one named last changes fastest.
Arguments:
- voxels: bfloat16 [24576, 512], P(('groups', 'space', 'sub')), parts along dimension 0, may hold values from -6 to 6
- window_ids: int32 [24576], P(('groups', 'space', 'sub')), parts along dimension 0, may hold values from 0 to 127, as said below
- voxel_slots: int32 [24576], P(('groups', 'space', 'sub')), parts along dimension 0, may hold values from 0 to 255, as said below
- window_counts: int32 [256], P('groups'), parts along dimension 0, may hold values from 0 to 256, as said below
- norm_gain: float32 [512], replicated, may hold values from 0.25 to 1.75
- w_query_key: bfloat16 [2, 512, 512], P(None, None, 'mp'), may hold values from -2 to 2
- w_value: bfloat16 [512, 512], P(None, 'mp'), may hold values from -0.25 to 0.25
- w_out: bfloat16 [512, 512], P('mp'), may hold values from -0.25 to 0.25
- ffn_gain: float32 [512], replicated, may hold values from 0.25 to 1.75
- w_up: bfloat16 [512, 2048], P(None, 'mp'), may hold values from -0.25 to 0.25
- w_down: bfloat16 [2048, 512], P('mp'), may hold values from -0.125 to 0.125
Outputs:
- result: bfloat16 [24576, 512], P(('groups', 'space', 'sub'), 'mp'), parts along dimension 0
There are 2 independent parts, one for each index of `groups`. A program takes and returns all parts, laid end to end along the dimension named above; an argument that names none is the same for every part. Nothing has to cross between parts.
Inputs may be any that keep to these rules, and one draw needn't show every extreme that they name: `window_ids`: window w belongs to owner w // 16 (its index along space+sub) as that owner's window w % 16. On the voxels of one device at most 384 lie in windows of one owner, and in every draw some owner has exactly 384 voxels of every device. `voxel_slots`: the voxels of a window hold slots 0 to its count - 1, each once. window_counts[w] is the number of voxels with window id w; some window holds 256.
All inputs are finite; a program needn't handle non-finite values.
Results may differ from a plain program's by a relative error of at most 0.012.
Values may be sent and summed in bfloat16 or wider, within the bound.
A program may use at most 128 MiB of HBM per device.

v0:
```python
import jax
import jax.numpy as jnp
from jax import lax
from jax.sharding import PartitionSpec as P

HDIM = 64
WLEN = 256
WIN_DEV = 16


def normalize(values_in, gain):
    row_mean = jnp.mean(values_in, axis=-1, keepdims=True)
    centred = values_in - row_mean
    variance = jnp.mean(centred * centred, axis=-1, keepdims=True)
    return centred * lax.rsqrt(variance + 1e-05) * gain


def project(rows_in, weight):
    return jnp.dot(rows_in, weight, preferred_element_type=jnp.float32).astype(jnp.bfloat16)


def feed_forward(normed_in, up_proj, down_proj):
    hidden = jax.nn.gelu(
        jnp.dot(normed_in, up_proj, preferred_element_type=jnp.float32), approximate=True
    ).astype(jnp.bfloat16)
    return jnp.dot(hidden, down_proj, preferred_element_type=jnp.float32)


def regroup(send_rows, send_spots):
    return (
        lax.all_to_all(send_rows, ("space", "sub"), split_axis=0, concat_axis=0, tiled=True),
        lax.all_to_all(send_spots, ("space", "sub"), split_axis=0, concat_axis=0, tiled=True),
    )


def send_back(send_rows):
    return lax.all_to_all(send_rows, ("space", "sub"), split_axis=0, concat_axis=0, tiled=True)


def attend(queries, key_rows, values, counts):
    windows = counts.shape[0]
    window_len = queries.shape[0] // windows
    head_count = queries.shape[1] // HDIM
    split_shape = (windows, window_len, head_count, HDIM)
    scores = jnp.einsum(
        "wqhd,wkhd->whqk",
        queries.reshape(split_shape),
        key_rows.reshape(split_shape),
        preferred_element_type=jnp.float32,
    ) * HDIM ** (-0.5)
    live_keys = (jnp.arange(window_len, dtype=jnp.int32)[None, :] < counts[:, None])[
        :, None, None, :
    ]
    scores = jnp.where(live_keys, scores, jnp.float32(-1e30))
    row_max = jnp.max(scores, axis=-1, keepdims=True)
    weights = jnp.exp(scores - row_max)
    probabilities = (weights / jnp.sum(weights, axis=-1, keepdims=True)).astype(jnp.bfloat16)
    mixture = jnp.einsum(
        "whqk,wkhd->wqhd",
        probabilities,
        values.reshape(split_shape),
        preferred_element_type=jnp.float32,
    )
    return mixture.astype(jnp.bfloat16).reshape(windows * window_len, head_count * HDIM)


def shards(
    voxels,
    window_ids,
    voxel_slots,
    window_counts,
    norm_gain,
    w_query_key,
    w_value,
    w_out,
    ffn_gain,
    w_up,
    w_down,
):
    owner_total = lax.axis_size(("space", "sub"))
    my_index = lax.axis_index(("space", "sub"))
    row_count = voxels.shape[0]
    capacity = 2 * row_count // owner_total
    local_width = w_value.shape[1]
    stream = voxels.astype(jnp.float32)
    normed = normalize(stream, norm_gain).astype(jnp.bfloat16)
    destination = window_ids // WIN_DEV
    position = window_ids % WIN_DEV * WLEN + voxel_slots
    target = (destination[:, None] == jnp.arange(owner_total, dtype=jnp.int32)[None, :]).astype(
        jnp.int32
    )
    before = jnp.sum((jnp.cumsum(target, axis=0) - target) * target, axis=1)
    send_index = destination * capacity + before
    row_width = normed.shape[1]
    outgoing = (
        jnp.zeros((owner_total * capacity, row_width), jnp.bfloat16).at[send_index].set(normed)
    )
    out_spots = (
        jnp.full((owner_total * capacity,), WIN_DEV * WLEN, jnp.int32).at[send_index].set(position)
    )
    arrived, arrived_spots = regroup(
        outgoing.reshape(owner_total, capacity, row_width), out_spots.reshape(owner_total, capacity)
    )
    arrived = arrived.reshape(owner_total * capacity, row_width)
    arrived_spots = arrived_spots.reshape(owner_total * capacity)
    padded = (
        jnp.zeros((WIN_DEV * WLEN, row_width), jnp.bfloat16)
        .at[arrived_spots]
        .set(arrived, mode="drop")
    )
    queries = project(padded, w_query_key[0])
    key_rows = project(padded, w_query_key[1])
    values = project(padded, w_value)
    counts = lax.dynamic_slice_in_dim(window_counts, my_index * WIN_DEV, WIN_DEV, 0)
    mixture = attend(queries, key_rows, values, counts)
    answer = jnp.take(mixture, arrived_spots, axis=0, mode="clip").reshape(
        owner_total, capacity, local_width
    )
    answer = send_back(answer)
    attended = answer.reshape(owner_total * capacity, local_width)[send_index]
    head_rows = w_out.shape[0]
    all_heads, whole_out = (
        lax.all_gather(attended, "mp", axis=1, tiled=True),
        lax.all_gather(w_out, "mp", axis=0, tiled=True),
    )
    after_attn = stream + jnp.dot(all_heads, whole_out, preferred_element_type=jnp.float32)
    ffn_terms = feed_forward(normalize(after_attn, ffn_gain).astype(jnp.bfloat16), w_up, w_down)
    remainder = lax.dynamic_slice_in_dim(after_attn, lax.axis_index("mp") * head_rows, head_rows, 1)
    result = (
        lax.psum_scatter(
            ffn_terms.astype(jnp.bfloat16), "mp", scatter_dimension=1, tiled=True
        ).astype(jnp.float32)
        + remainder
    )
    return result.astype(jnp.bfloat16)


def solution(mesh):
    return jax.shard_map(
        shards,
        mesh=mesh,
        in_specs=(
            P(("groups", "space", "sub"), None),
            P(("groups", "space", "sub")),
            P(("groups", "space", "sub")),
            P("groups"),
            P(),
            P(None, None, "mp"),
            P(None, "mp"),
            P("mp", None),
            P(),
            P(None, "mp"),
            P("mp", None),
        ),
        out_specs=P(("groups", "space", "sub"), "mp"),
        check_vma=False,
    )
```

profile of v0, /device:TPU:0, one launch (start us, length us, event | category | flops | bytes accessed | tf_op | source)
XLA Modules:
  0.0 341.2 jit_solution(189395623815067375)
XLA Ops:
  7.4 2.3 reduce-window.6
  10.3 6.8 %scatter_custom_fusion = s32[3072]{0:T(1024)} fusion(s32[1536]{0:T(1024)S(1)} %compare_select_fusion.1, s32[1536]{0:T(1024)S(1)} %get-tuple-element.5, s32[]{:T(128)} %constant.31.clone.1), kind=kCustom, calls=%fused_computation.79 | custom fusion | bytes 12292 | tf_op jit(solution)/shard_map/scatter | solution.py:99
  17.0 6.4 %all-to-all-start = ((s32[8,1,384]{2,1,0:T(1,128)}), s32[8,1,384]{2,1,0:T(1,128)S(1)}, u32[]{:S(2)}, u32[]{:S(2)}) async-start(s32[8,1,384]{2,1,0:T(1,128)} %bitcast.2), calls=%async_computation | async-start | bytes 24576 | tf_op jit(solution)/shard_map/all_to_all | solution.py:32
  23.4 1.7 copy.19
  25.8 1.6 fusion.22
  27.5 2.6 copy.20
  30.1 9.9 %scatter_custom_fusion.1 = bf16[3072,512]{1,0:T(8,128)(2,1)} fusion(s32[1536]{0:T(1024)S(1)} %compare_select_fusion.1, bf16[1536,512]{1,0:T(8,128)(2,1)} %copy.20, bf16[]{:T(256)} %constant.28.clone.1), kind=kCustom, calls=%fused_computation.48 | custom fusion | bytes 3146240 | tf_op jit(solution)/shard_map/scatter | solution.py:96
  40.0 5.2 %all-to-all-start.1 = ((bf16[8,384,512]{2,1,0:T(8,128)(2,1)}), bf16[8,384,512]{2,1,0:T(8,128)(2,1)}, u32[]{:S(2)}, u32[]{:S(2)}) async-start(bf16[8,384,512]{2,1,0:T(8,128)(2,1)} %bitcast.45), calls=%async_computation.1 | async-start | bytes 6291456 | tf_op jit(solution)/shard_map/all_to_all | solution.py:31
  45.4 71.4 %all-to-all-done.1 = bf16[8,384,512]{2,1,0:T(8,128)(2,1)} async-done(((bf16[8,384,512]{2,1,0:T(8,128)(2,1)}), bf16[8,384,512]{2,1,0:T(8,128)(2,1)}, u32[]{:S(2)}, u32[]{:S(2)}) %all-to-all-start.1) | async-done | bytes 3145760 | tf_op jit(solution)/shard_map/all_to_all | solution.py:31
  116.8 16.9 %scatter_custom_fusion.2 = bf16[4096,512]{1,0:T(8,128)(2,1)} fusion(s32[3072]{0:T(1024)S(1)} %bitcast.51, bf16[3072,512]{1,0:T(8,128)(2,1)} %bitcast.6, bf16[]{:T(256)} %constant.28.clone.1), kind=kCustom, calls=%fused_computation.42 | custom fusion | bytes 4194816 | tf_op jit(solution)/shard_map/scatter | solution.py:109
  133.7 4.9 %convolution_convert_fusion.1 = bf16[4096,256]{1,0:T(8,128)(2,1)} fusion(bf16[4096,512]{1,0:T(8,128)(2,1)} %scatter_custom_fusion.2, bf16[2,512,256]{2,1,0:T(8,128)(2,1)S(1)} %copy-done.7), kind=kOutput, calls=%fused_computation.24 | convolution fusion | flops 1074790400 | bytes 6553600 | tf_op jit(solution)/shard_map/dot_general | solution.py:19
  138.6 1.3 convolution_convert_fusion
  139.9 7.1 %reshape.179 = bf16[16,256,4,64]{3,2,1,0:T(4,128)(2,1)} reshape(bf16[4096,256]{1,0:T(8,128)(2,1)} %convolution_convert_fusion.1) | data formatting | bytes 4194304 | tf_op jit(solution)/shard_map/reshape | solution.py:47
  147.0 3.2 reshape.180
  150.2 3.4 %convolution_convert_fusion.2 = bf16[4096,256]{1,0:T(8,128)(2,1)S(1)} fusion(bf16[4096,512]{1,0:T(8,128)(2,1)} %scatter_custom_fusion.2, bf16[512,256]{1,0:T(8,128)(2,1)S(1)} %copy-done.9), kind=kOutput, calls=%fused_computation.25 | convolution fusion | flops 1074790400 | bytes 6553600 | tf_op jit(solution)/shard_map/dot_general | solution.py:19
  153.6 3.3 reshape.178
  156.9 11.5 %fusion.14 = f32[16,4,256,256]{2,3,1,0:T(8,128)} fusion(bf16[16,256,4,64]{3,2,1,0:T(4,128)(2,1)} %reshape.180, bf16[16,256,4,64]{3,2,1,0:T(4,128)(2,1)} %reshape.179), kind=kOutput, calls=%fused_computation.29 | convolution fusion | flops 536870912 | bytes 20971520 | tf_op jit(solution)/shard_map/wqhd,wkhd->whqk/dot_general | solution.py:45
  168.4 18.8 %fusion.52 = (f32[16,4,256]{2,1,0:T(4,128)S(1)}, f32[16,4,256,256]{2,3,1,0:T(8,128)}) fusion(f32[16,4,256,256]{2,3,1,0:T(8,128)} %fusion.14, pred[16,256]{1,0:T(8,128)(4,1)S(1)} %iota_compare_fusion.2), kind=kOutput, calls=%fused_computation.90 | output fusion | flops 25166080 | bytes 33624064 | tf_op jit(solution)/shard_map/sub | solution.py:56
  187.2 9.0 %convert_bitcast_fusion = bf16[16,256,4,64]{1,3,2,0:T(8,128)(2,1)S(1)} fusion(f32[16,4,256,256]{2,3,1,0:T(8,128)} %get-tuple-element.8, f32[16,4,256]{2,1,0:T(4,128)S(1)} %get-tuple-element.7, bf16[16,256,4,64]{3,2,1,0:T(4,128)(2,1)} %reshape.178), kind=kOutput, calls=%fused_computation.41 | convolution fusion | flops 546308096 | bytes 21037056 | tf_op jit(solution)/shard_map/whqk,wkhd->wqhd/dot_general | solution.py:58
  196.2 4.6 %copy.40 = bf16[16,256,4,64]{3,2,1,0:T(4,128)(2,1)} copy(bf16[16,256,4,64]{1,3,2,0:T(8,128)(2,1)S(1)} %convert_bitcast_fusion) | data formatting | bytes 4194304 | tf_op jit(solution)/shard_map/reshape | solution.py:64
  200.8 6.0 %reshape.181 = bf16[4096,256]{1,0:T(8,128)(2,1)S(1)} reshape(bf16[16,256,4,64]{3,2,1,0:T(4,128)(2,1)} %copy.40) | data formatting | bytes 4194304 | tf_op jit(solution)/shard_map/reshape | solution.py:64
  206.8 13.0 %gather_fusion = bf16[3072,256]{1,0:T(8,128)(2,1)} fusion(bf16[4096,256]{1,0:T(8,128)(2,1)S(1)} %reshape.181, s32[3072]{0:T(1024)S(1)} %broadcast_clamp_fusion), kind=kCustom, calls=%fused_computation | custom fusion | bytes 3158016 | tf_op jit(solution)/shard_map/jit(_take)/gather | solution.py:116
  219.8 3.6 %all-to-all-start.2 = ((bf16[8,384,256]{2,1,0:T(8,128)(2,1)}), bf16[8,384,256]{2,1,0:T(8,128)(2,1)S(1)}, u32[]{:S(2)}, u32[]{:S(2)}) async-start(bf16[8,384,256]{2,1,0:T(8,128)(2,1)} %bitcast.46), calls=%async_computation.2 | async-start | bytes 3145728 | tf_op jit(solution)/shard_map/all_to_all | solution.py:37
  223.4 37.7 %all-to-all-done.2 = bf16[8,384,256]{2,1,0:T(8,128)(2,1)S(1)} async-done(((bf16[8,384,256]{2,1,0:T(8,128)(2,1)}), bf16[8,384,256]{2,1,0:T(8,128)(2,1)S(1)}, u32[]{:S(2)}, u32[]{:S(2)}) %all-to-all-start.2) | async-done | bytes 1572896 | tf_op jit(solution)/shard_map/all_to_all | solution.py:37
  261.1 5.4 %gather_fusion.1 = bf16[1536,256]{1,0:T(8,128)(2,1)} fusion(bf16[3072,256]{1,0:T(8,128)(2,1)S(1)} %bitcast.44, s32[2048]{0:T(1024)S(1)} %pad_clamp_fusion), kind=kCustom, calls=%fused_computation.1 | custom fusion | bytes 1579008 | tf_op jit(solution)/shard_map/gather | solution.py:120
  266.5 8.4 %all_gather.7 = bf16[512,512]{1,0:T(8,128)(2,1)S(1)} all-gather(bf16[256,512]{1,0:T(8,128)(2,1)S(1)} %copy-done.4), channel_id=1, replica_groups=mesh['groups'=2,'space'=4,'mp'=2,'sub'=2] {'mp'}, dimensions={0}, use_global_device_ids=true | all-gather | bytes 786432 | tf_op jit(solution)/shard_map/all_gather | solution.py:124
  274.9 17.7 %all-gather.3.cloned.1.call-done = bf16[1536,512]{1,0:T(8,128)(2,1)} async-done(((bf16[1536,256]{1,0:T(8,128)(2,1)}), bf16[1536,512]{1,0:T(8,128)(2,1)}) %all-gather.3.cloned.1.call-update) | async-done | bytes 1572880 | tf_op jit(solution)/shard_map/all_gather | solution.py:123
  292.7 2.9 fusion.53
  295.7 1.6 copy-done.2
  297.8 7.4 %convolution_convert_fusion.3 = bf16[1536,512]{0,1:T(8,128)(2,1)} fusion(bf16[1024,512]{1,0:T(8,128)(2,1)S(1)} %copy-done, bf16[512,1024]{1,0:T(8,128)(2,1)S(1)} %copy-done.6, f32[1536,512]{0,1:T(8,128)} %copy-done.2, f32[512]{0:T(512)S(1)} %copy-done.10, f32[1536]{0:T(1024)S(1)} %add_rsqrt_fusion, f32[1536]{0:T(1024)S(1)} %broadcast_multiply_fusion), kind=kOutput, calls=%fused_computation.40 | convolution fusion | flops 3239313408 | bytes 6830080 | tf_op jit(solution)/shard_map/dot_general | solution.py:26
  305.2 26.3 %reduce-scatter.2.cloned.1.call-done = bf16[1536,256]{0,1:T(8,128)(2,1)} async-done(((bf16[1536,512]{0,1:T(8,128)(2,1)}), bf16[1536,256]{0,1:T(8,128)(2,1)}) %reduce-scatter.2.cloned.1.call-update) | async-done | bytes 786448 | tf_op jit(solution)/shard_map/reduce_scatter | solution.py:130
  331.5 1.8 add_convert_fusion
  (48 shorter events, 4.1 us)
Async XLA Ops:
  6.5 291.2 %copy-start = (bf16[1024,512]{1,0:T(8,128)(2,1)S(1)}, bf16[1024,512]{1,0:T(8,128)(2,1)}, u32[]{:S(2)}) copy-start(bf16[1024,512]{1,0:T(8,128)(2,1)} %param.21) | copy-start | bytes 3145732
  17.0 23.0 %all-to-all-start = ((s32[8,1,384]{2,1,0:T(1,128)}), s32[8,1,384]{2,1,0:T(1,128)S(1)}, u32[]{:S(2)}, u32[]{:S(2)}) async-start(s32[8,1,384]{2,1,0:T(1,128)} %bitcast.2), calls=%async_computation | async-start | bytes 24576 | tf_op jit(solution)/shard_map/all_to_all | solution.py:32
  23.4 2.5 copy-start.5
  25.1 2.4 copy-start.1
  40.0 5.2 %copy-start.11 = (s32[128]{0:T(128)S(1)}, s32[128]{0:T(128)}, u32[]{:S(2)}) copy-start(s32[128]{0:T(128)} %param.14) | copy-start | bytes 1540
  40.0 76.8 %all-to-all-start.1 = ((bf16[8,384,512]{2,1,0:T(8,128)(2,1)}), bf16[8,384,512]{2,1,0:T(8,128)(2,1)}, u32[]{:S(2)}, u32[]{:S(2)}) async-start(bf16[8,384,512]{2,1,0:T(8,128)(2,1)} %bitcast.45), calls=%async_computation.1 | async-start | bytes 6291456 | tf_op jit(solution)/shard_map/all_to_all | solution.py:31
  45.2 88.5 %copy-start.7 = (bf16[2,512,256]{2,1,0:T(8,128)(2,1)S(1)}, bf16[2,512,256]{2,1,0:T(8,128)(2,1)}, u32[]{:S(2)}) copy-start(bf16[2,512,256]{2,1,0:T(8,128)(2,1)} %param.16) | copy-start | bytes 1572868
  133.7 4.9 %copy-start.3 = (bf16[4096,512]{1,0:T(8,128)(2,1)S(1)}, bf16[4096,512]{1,0:T(8,128)(2,1)}, u32[]{:S(2)}) copy-start(bf16[4096,512]{1,0:T(8,128)(2,1)} %scatter_custom_fusion.2) | copy-start | bytes 12582916
  133.7 4.9 %copy-start.8 = (bf16[2,512,256]{2,1,0:T(8,128)(2,1)S(1)}, bf16[2,512,256]{2,1,0:T(8,128)(2,1)}, u32[]{:S(2)}) copy-start(bf16[2,512,256]{2,1,0:T(8,128)(2,1)} %param.16) | copy-start | bytes 1572868
  147.0 3.2 copy-start.9
  219.8 41.3 %all-to-all-start.2 = ((bf16[8,384,256]{2,1,0:T(8,128)(2,1)}), bf16[8,384,256]{2,1,0:T(8,128)(2,1)S(1)}, u32[]{:S(2)}, u32[]{:S(2)}) async-start(bf16[8,384,256]{2,1,0:T(8,128)(2,1)} %bitcast.46), calls=%async_computation.2 | async-start | bytes 3145728 | tf_op jit(solution)/shard_map/all_to_all | solution.py:37
  223.4 69.3 %all-gather.3.cloned.1.call-start = ((), (), s32[]{:S(2)}) async-start(), calls=%async_computation.5 | async-start | bytes 2359296 | tf_op jit(solution)/shard_map/all_gather | solution.py:123
  261.1 5.4 %copy-start.4 = (bf16[256,512]{1,0:T(8,128)(2,1)S(1)}, bf16[256,512]{1,0:T(8,128)(2,1)}, u32[]{:S(2)}) copy-start(bf16[256,512]{1,0:T(8,128)(2,1)} %param.18) | copy-start | bytes 786436
  266.5 65.0 %reduce-scatter.2.cloned.1.call-start = ((), (), s32[]{:S(2)}) async-start(), calls=%async_computation.4 | async-start | bytes 2359296 | tf_op jit(solution)/shard_map/reduce_scatter | solution.py:130
  295.6 1.7 copy-start.2
  295.7 2.1 copy-start.6
  295.7 2.1 copy-start.10
Sparse Core Ops, SparseCore 0:
  266.6 26.0 all-gather.2
  305.3 26.1 reduce-scatter.1
where the time goes:
time: 342 us; the launch traced here: 341 us
  waiting for transfers between devices  153 us (45%)
  local copies, waits for them, and re-layouts  83.5 us (24%)
  matrix products  40.4 us (12%)
  other arithmetic  26.9 us (8%)
  starting transfers between devices  15.2 us (4%)
  between operations  13.6 us (4%)
  blocking collectives  8.42 us (2%)
    all_to_all x1, waiting for transfers between devices, regroup(): lax.all_to_all(send_rows, ('space', 'sub'), split_axis=0, concat_axis=0,...  71.4 us
    all_to_all x1, waiting for transfers between devices, send_back(): lax.all_to_all(send_rows, ('space', 'sub'), split_axis=0, concat_axis=0,...  37.7 us
    reduce_scatter x1, waiting for transfers between devices, shards(): lax.psum_scatter(ffn_terms.astype(jnp.bfloat16), 'mp', scatter_dimension=...  26.3 us
    sub x1, other arithmetic, attend(): weights = jnp.exp(scores - row_max)  18.8 us
    all_gather x1, waiting for transfers between devices, shards(): lax.all_gather(attended, 'mp', axis=1, tiled=True)  17.7 us
    scatter x1, local copies, waits for them, and re-layouts, shards(): padded = jnp.zeros((WIN_DEV * WLEN, row_width), jnp.bfloat16).at[arrived_...  16.9 us
    gather x1, local copies, waits for them, and re-layouts, shards(): jnp.take(mixture, arrived_spots, axis=0, mode='clip')  13 us
    dot_general x1, matrix products, attend(): jnp.einsum('wqhd,wkhd->whqk', queries.reshape(split_shape), key_rows.resh...  11.5 us
  transfers between devices with their start and end apart: 5, of which 4 were waited for; matrix products, arithmetic and copies ran while one was open for 5% of the time, Pallas kernels for 0%

commit v1 on v0

--- a/solution.py
+++ b/solution.py
@@ -6,6 +6,18 @@
 HDIM = 64
 WLEN = 256
 WIN_DEV = 16
+
+
+def collect(x, axis, dim):
+    ways, here = (lax.axis_size(axis), lax.axis_index(axis))
+    grown, reach = (x, 1)
+    while reach < ways:
+        theirs = lax.ppermute(grown, axis, [(d, d ^ reach) for d in range(ways)])
+        mine_first = jnp.concatenate([grown, theirs], axis=dim)
+        theirs_first = jnp.concatenate([theirs, grown], axis=dim)
+        grown = jnp.where(here & reach == 0, mine_first, theirs_first)
+        reach = 2 * reach
+    return grown
 
 
 def normalize(values_in, gain):
@@ -120,7 +132,7 @@
     attended = answer.reshape(owner_total * capacity, local_width)[send_index]
     head_rows = w_out.shape[0]
     all_heads, whole_out = (
-        lax.all_gather(attended, "mp", axis=1, tiled=True),
+        collect(attended, "mp", 1),
         lax.all_gather(w_out, "mp", axis=0, tiled=True),
     )
     after_attn = stream + jnp.dot(all_heads, whole_out, preferred_element_type=jnp.float32)

time: 342 us -> 339 us (level)
  waiting for transfers between devices: 153 us -> 135 us
  blocking collectives: 8.42 us -> 23.1 us
    all_gather x1 -> x0, waiting for transfers between devices: 17.7 us -> none  [shards(): lax.all_gather(attended, 'mp', axis=1, tiled=True)]
    all_gather x1, blocking collectives: 8.42 us -> 23.1 us  [shards(): lax.all_gather(w_out, 'mp', axis=0, tiled=True)]
  transfers between devices with their start and end apart: 5 -> 5, of which waited for: 4 -> 3; matrix products, arithmetic and copies ran while one was open for 5% -> 5% of each run, Pallas kernels for 0% -> 0%
where the time goes in v1:
time: 339 us; the launch traced here: 338 us
  waiting for transfers between devices  135 us (40%)
  local copies, waits for them, and re-layouts  82.9 us (24%)
  matrix products  40 us (12%)
  other arithmetic  26.9 us (8%)
  blocking collectives  23.1 us (7%)
  starting transfers between devices  16.8 us (5%)
  between operations  13.6 us (4%)
    all_to_all x1, waiting for transfers between devices, regroup(): lax.all_to_all(send_rows, ('space', 'sub'), split_axis=0, concat_axis=0,...  71.4 us
    all_to_all x1, waiting for transfers between devices, send_back(): lax.all_to_all(send_rows, ('space', 'sub'), split_axis=0, concat_axis=0,...  37.7 us
    reduce_scatter x1, waiting for transfers between devices, shards(): lax.psum_scatter(ffn_terms.astype(jnp.bfloat16), 'mp', scatter_dimension=...  25.7 us
    all_gather x1, blocking collectives, shards(): lax.all_gather(w_out, 'mp', axis=0, tiled=True)  23.1 us
    sub x1, other arithmetic, attend(): weights = jnp.exp(scores - row_max)  18.8 us
    scatter x1, local copies, waits for them, and re-layouts, shards(): padded = jnp.zeros((WIN_DEV * WLEN, row_width), jnp.bfloat16).at[arrived_...  16.9 us
    gather x1, local copies, waits for them, and re-layouts, shards(): jnp.take(mixture, arrived_spots, axis=0, mode='clip')  13 us
    dot_general x1, matrix products, attend(): jnp.einsum('wqhd,wkhd->whqk', queries.reshape(split_shape), key_rows.resh...  11.5 us
  transfers between devices with their start and end apart: 5, of which 3 were waited for; matrix products, arithmetic and copies ran while one was open for 5% of the time, Pallas kernels for 0%

profile of v1, /device:TPU:0, one launch (start us, length us, event | category | flops | bytes accessed | tf_op | source)
XLA Modules:
  0.0 338.1 jit_solution(14662303979921644954)
XLA Ops:
  7.4 2.3 reduce-window.6
  10.3 6.8 %scatter_custom_fusion = s32[3072]{0:T(1024)} fusion(s32[1536]{0:T(1024)S(1)} %compare_select_fusion.1, s32[1536]{0:T(1024)S(1)} %get-tuple-element.5, s32[]{:T(128)} %constant.34.clone.1), kind=kCustom, calls=%fused_computation.86 | custom fusion | bytes 12292 | tf_op jit(solution)/shard_map/scatter | solution.py:111
  17.0 6.4 %all-to-all-start = ((s32[8,1,384]{2,1,0:T(1,128)}), s32[8,1,384]{2,1,0:T(1,128)S(1)}, u32[]{:S(2)}, u32[]{:S(2)}) async-start(s32[8,1,384]{2,1,0:T(1,128)} %bitcast.2), calls=%async_computation | async-start | bytes 24576 | tf_op jit(solution)/shard_map/all_to_all | solution.py:44
  23.4 1.7 copy.19
  25.8 1.6 fusion.22
  27.5 2.6 copy.20
  30.1 9.9 %scatter_custom_fusion.1 = bf16[3072,512]{1,0:T(8,128)(2,1)} fusion(s32[1536]{0:T(1024)S(1)} %compare_select_fusion.1, bf16[1536,512]{1,0:T(8,128)(2,1)} %copy.20, bf16[]{:T(256)} %constant.33.clone.1), kind=kCustom, calls=%fused_computation.54 | custom fusion | bytes 3146240 | tf_op jit(solution)/shard_map/scatter | solution.py:108
  40.0 5.2 %all-to-all-start.1 = ((bf16[8,384,512]{2,1,0:T(8,128)(2,1)}), bf16[8,384,512]{2,1,0:T(8,128)(2,1)}, u32[]{:S(2)}, u32[]{:S(2)}) async-start(bf16[8,384,512]{2,1,0:T(8,128)(2,1)} %bitcast.44), calls=%async_computation.1 | async-start | bytes 6291456 | tf_op jit(solution)/shard_map/all_to_all | solution.py:43
  45.4 71.4 %all-to-all-done.1 = bf16[8,384,512]{2,1,0:T(8,128)(2,1)} async-done(((bf16[8,384,512]{2,1,0:T(8,128)(2,1)}), bf16[8,384,512]{2,1,0:T(8,128)(2,1)}, u32[]{:S(2)}, u32[]{:S(2)}) %all-to-all-start.1) | async-done | bytes 3145760 | tf_op jit(solution)/shard_map/all_to_all | solution.py:43
  116.8 16.9 %scatter_custom_fusion.2 = bf16[4096,512]{1,0:T(8,128)(2,1)} fusion(s32[3072]{0:T(1024)S(1)} %bitcast.50, bf16[3072,512]{1,0:T(8,128)(2,1)} %bitcast.6, bf16[]{:T(256)} %constant.33.clone.1), kind=kCustom, calls=%fused_computation.42 | custom fusion | bytes 4194816 | tf_op jit(solution)/shard_map/scatter | solution.py:121
  133.7 4.9 %convolution_convert_fusion.1 = bf16[4096,256]{1,0:T(8,128)(2,1)} fusion(bf16[4096,512]{1,0:T(8,128)(2,1)} %scatter_custom_fusion.2, bf16[2,512,256]{2,1,0:T(8,128)(2,1)S(1)} %copy-done.6), kind=kOutput, calls=%fused_computation.24 | convolution fusion | flops 1074790400 | bytes 6553600 | tf_op jit(solution)/shard_map/dot_general | solution.py:31
  138.6 1.3 convolution_convert_fusion
  139.9 7.1 %reshape.178 = bf16[16,256,4,64]{3,2,1,0:T(4,128)(2,1)} reshape(bf16[4096,256]{1,0:T(8,128)(2,1)} %convolution_convert_fusion.1) | data formatting | bytes 4194304 | tf_op jit(solution)/shard_map/reshape | solution.py:59
  147.0 3.2 reshape.179
  150.2 3.4 %convolution_convert_fusion.2 = bf16[4096,256]{1,0:T(8,128)(2,1)S(1)} fusion(bf16[4096,512]{1,0:T(8,128)(2,1)} %scatter_custom_fusion.2, bf16[512,256]{1,0:T(8,128)(2,1)S(1)} %copy-done.8), kind=kOutput, calls=%fused_computation.25 | convolution fusion | flops 1074790400 | bytes 6553600 | tf_op jit(solution)/shard_map/dot_general | solution.py:31
  153.6 3.3 reshape.177
  156.9 11.5 %fusion.14 = f32[16,4,256,256]{2,3,1,0:T(8,128)} fusion(bf16[16,256,4,64]{3,2,1,0:T(4,128)(2,1)} %reshape.179, bf16[16,256,4,64]{3,2,1,0:T(4,128)(2,1)} %reshape.178), kind=kOutput, calls=%fused_computation.29 | convolution fusion | flops 536870912 | bytes 20971520 | tf_op jit(solution)/shard_map/wqhd,wkhd->whqk/dot_general | solution.py:57
  168.4 18.8 %fusion.59 = (f32[16,4,256]{2,1,0:T(4,128)S(1)}, f32[16,4,256,256]{2,3,1,0:T(8,128)}) fusion(f32[16,4,256,256]{2,3,1,0:T(8,128)} %fusion.14, pred[16,256]{1,0:T(8,128)(4,1)S(1)} %iota_compare_fusion.2), kind=kOutput, calls=%fused_computation.98 | output fusion | flops 25166080 | bytes 33624064 | tf_op jit(solution)/shard_map/sub | solution.py:68
  187.2 9.0 %convert_bitcast_fusion = bf16[16,256,4,64]{1,3,2,0:T(8,128)(2,1)S(1)} fusion(f32[16,4,256,256]{2,3,1,0:T(8,128)} %get-tuple-element.8, f32[16,4,256]{2,1,0:T(4,128)S(1)} %get-tuple-element.7, bf16[16,256,4,64]{3,2,1,0:T(4,128)(2,1)} %reshape.177), kind=kOutput, calls=%fused_computation.41 | convolution fusion | flops 546308096 | bytes 21037056 | tf_op jit(solution)/shard_map/whqk,wkhd->wqhd/dot_general | solution.py:70
  196.2 4.6 %copy.40 = bf16[16,256,4,64]{3,2,1,0:T(4,128)(2,1)} copy(bf16[16,256,4,64]{1,3,2,0:T(8,128)(2,1)S(1)} %convert_bitcast_fusion) | data formatting | bytes 4194304 | tf_op jit(solution)/shard_map/reshape | solution.py:76
  200.8 6.0 %reshape.180 = bf16[4096,256]{1,0:T(8,128)(2,1)S(1)} reshape(bf16[16,256,4,64]{3,2,1,0:T(4,128)(2,1)} %copy.40) | data formatting | bytes 4194304 | tf_op jit(solution)/shard_map/reshape | solution.py:76
  206.8 13.0 %gather_fusion = bf16[3072,256]{1,0:T(8,128)(2,1)} fusion(bf16[4096,256]{1,0:T(8,128)(2,1)S(1)} %reshape.180, s32[3072]{0:T(1024)S(1)} %broadcast_clamp_fusion), kind=kCustom, calls=%fused_computation | custom fusion | bytes 3158016 | tf_op jit(solution)/shard_map/jit(_take)/gather | solution.py:128
  219.8 3.6 %all-to-all-start.2 = ((bf16[8,384,256]{2,1,0:T(8,128)(2,1)}), bf16[8,384,256]{2,1,0:T(8,128)(2,1)S(1)}, u32[]{:S(2)}, u32[]{:S(2)}) async-start(bf16[8,384,256]{2,1,0:T(8,128)(2,1)} %bitcast.45), calls=%async_computation.2 | async-start | bytes 3145728 | tf_op jit(solution)/shard_map/all_to_all | solution.py:49
  223.4 37.7 %all-to-all-done.2 = bf16[8,384,256]{2,1,0:T(8,128)(2,1)S(1)} async-done(((bf16[8,384,256]{2,1,0:T(8,128)(2,1)}), bf16[8,384,256]{2,1,0:T(8,128)(2,1)S(1)}, u32[]{:S(2)}, u32[]{:S(2)}) %all-to-all-start.2) | async-done | bytes 1572896 | tf_op jit(solution)/shard_map/all_to_all | solution.py:49
  261.1 4.8 %gather_fusion.1 = bf16[1536,256]{1,0:T(8,128)(2,1)S(1)} fusion(bf16[3072,256]{1,0:T(8,128)(2,1)S(1)} %bitcast.43, s32[2048]{0:T(1024)S(1)} %pad_clamp_fusion), kind=kCustom, calls=%fused_computation.1 | custom fusion | bytes 1579008 | tf_op jit(solution)/shard_map/gather | solution.py:132
  265.8 1.6 collective-permute-start
  267.4 23.1 %all_gather.3 = bf16[512,512]{1,0:T(8,128)(2,1)S(1)} all-gather(bf16[256,512]{1,0:T(8,128)(2,1)} %param.18), channel_id=1, replica_groups=mesh['groups'=2,'space'=4,'mp'=2,'sub'=2] {'mp'}, dimensions={0}, use_global_device_ids=true | all-gather | bytes 786432 | tf_op jit(solution)/shard_map/all_gather | solution.py:136
  290.5 2.6 fusion.60
  293.1 1.6 copy-done.2
  295.2 7.4 %convolution_convert_fusion.3 = bf16[1536,512]{0,1:T(8,128)(2,1)} fusion(bf16[1024,512]{1,0:T(8,128)(2,1)S(1)} %copy-done, bf16[512,1024]{1,0:T(8,128)(2,1)S(1)} %copy-done.5, f32[1536,512]{0,1:T(8,128)} %copy-done.2, f32[512]{0:T(512)S(1)} %copy-done.9, f32[1536]{0:T(1024)S(1)} %add_rsqrt_fusion, f32[1536]{0:T(1024)S(1)} %broadcast_multiply_fusion), kind=kOutput, calls=%fused_computation.40 | convolution fusion | flops 3239313408 | bytes 6830080 | tf_op jit(solution)/shard_map/dot_general | solution.py:38
  302.6 25.7 %reduce-scatter.2.cloned.1.call-done = bf16[1536,256]{0,1:T(8,128)(2,1)} async-done(((bf16[1536,512]{0,1:T(8,128)(2,1)}), bf16[1536,256]{0,1:T(8,128)(2,1)}) %reduce-scatter.2.cloned.1.call-update) | async-done | bytes 786448 | tf_op jit(solution)/shard_map/reduce_scatter | solution.py:142
  328.3 1.8 add_convert_fusion
  (45 shorter events, 4.0 us)
Async XLA Ops:
  6.5 288.6 %copy-start = (bf16[1024,512]{1,0:T(8,128)(2,1)S(1)}, bf16[1024,512]{1,0:T(8,128)(2,1)}, u32[]{:S(2)}) copy-start(bf16[1024,512]{1,0:T(8,128)(2,1)} %param.21) | copy-start | bytes 3145732
  17.0 23.0 %all-to-all-start = ((s32[8,1,384]{2,1,0:T(1,128)}), s32[8,1,384]{2,1,0:T(1,128)S(1)}, u32[]{:S(2)}, u32[]{:S(2)}) async-start(s32[8,1,384]{2,1,0:T(1,128)} %bitcast.2), calls=%async_computation | async-start | bytes 24576 | tf_op jit(solution)/shard_map/all_to_all | solution.py:44
  23.4 2.5 copy-start.4
  25.1 2.4 copy-start.1
  40.0 5.2 %copy-start.10 = (s32[128]{0:T(128)S(1)}, s32[128]{0:T(128)}, u32[]{:S(2)}) copy-start(s32[128]{0:T(128)} %param.14) | copy-start | bytes 1540
  40.0 76.8 %all-to-all-start.1 = ((bf16[8,384,512]{2,1,0:T(8,128)(2,1)}), bf16[8,384,512]{2,1,0:T(8,128)(2,1)}, u32[]{:S(2)}, u32[]{:S(2)}) async-start(bf16[8,384,512]{2,1,0:T(8,128)(2,1)} %bitcast.44), calls=%async_computation.1 | async-start | bytes 6291456 | tf_op jit(solution)/shard_map/all_to_all | solution.py:43
  45.2 88.5 %copy-start.6 = (bf16[2,512,256]{2,1,0:T(8,128)(2,1)S(1)}, bf16[2,512,256]{2,1,0:T(8,128)(2,1)}, u32[]{:S(2)}) copy-start(bf16[2,512,256]{2,1,0:T(8,128)(2,1)} %param.16) | copy-start | bytes 1572868
  133.7 4.9 %copy-start.3 = (bf16[4096,512]{1,0:T(8,128)(2,1)S(1)}, bf16[4096,512]{1,0:T(8,128)(2,1)}, u32[]{:S(2)}) copy-start(bf16[4096,512]{1,0:T(8,128)(2,1)} %scatter_custom_fusion.2) | copy-start | bytes 12582916
  133.7 4.9 %copy-start.7 = (bf16[2,512,256]{2,1,0:T(8,128)(2,1)S(1)}, bf16[2,512,256]{2,1,0:T(8,128)(2,1)}, u32[]{:S(2)}) copy-start(bf16[2,512,256]{2,1,0:T(8,128)(2,1)} %param.16) | copy-start | bytes 1572868
  147.0 3.2 copy-start.8
  219.8 41.3 %all-to-all-start.2 = ((bf16[8,384,256]{2,1,0:T(8,128)(2,1)}), bf16[8,384,256]{2,1,0:T(8,128)(2,1)S(1)}, u32[]{:S(2)}, u32[]{:S(2)}) async-start(bf16[8,384,256]{2,1,0:T(8,128)(2,1)} %bitcast.45), calls=%async_computation.2 | async-start | bytes 3145728 | tf_op jit(solution)/shard_map/all_to_all | solution.py:49
  223.4 105.0 %reduce-scatter.2.cloned.1.call-start = ((), (), s32[]{:S(2)}) async-start(), calls=%async_computation.4 | async-start | bytes 2359296 | tf_op jit(solution)/shard_map/reduce_scatter | solution.py:142
  265.8 24.7 %collective-permute-start = (bf16[1536,256]{1,0:T(8,128)(2,1)S(1)}, bf16[1536,256]{1,0:T(8,128)(2,1)S(1)}, u32[]{:S(2)}, u32[]{:S(2)}) collective-permute-start(bf16[1536,256]{1,0:T(8,128)(2,1)S(1)} %gather_fusion.1), channel_id=1, source_target_pairs={{0,2},{2,0},{1,3},{3,1},{4,6},{6,4},{5,7},{7,5},{8,10},{10,8},{9,1... | collective-permute-start | bytes 2359304 | tf_op jit(solution)/shard_map/ppermute | solution.py:15
  293.1 1.7 copy-start.2
  293.1 2.1 copy-start.5
  293.1 2.1 copy-start.9
Sparse Core Ops, SparseCore 0:
  302.7 25.5 reduce-scatter.1
